TPU v7x, 64 devices: a 2x2x8 block of a 4x4x8 slice. The times are simulated.
64 devices in a mesh: inst: 4 (over x, y), qx: 16 (over z, core).
Axes of the slice: x: 2, y: 2, z: 8, core: 2. Of those that a mesh axis runs over, the one named last changes fastest.
The devices are a block of a 4x4x8 slice.
Arguments:
- cost_diag: float32 [4194304], P(('inst', 'qx')), parts along dimension 0
- phase_angles: float32 [6], replicated
- mixer_angles: float32 [6], replicated
Outputs:
- output 1: float32 [4], P('inst'), parts along dimension 0
- output 2: float32 [48], P('inst'), parts along dimension 0
- output 3: float32 [4194304], P(('inst', 'qx')), parts along dimension 0
- output 4: float32 [4194304], P(('inst', 'qx')), parts along dimension 0
There are 4 independent parts. A program takes and returns all parts, laid end to end along the dimension named above; an argument that names none is the same for every part.
All inputs are finite; a program needn't handle non-finite values.
Results may differ from a plain program's by a relative error of at most 0.001.
Values sent between devices are 32-bit elements.
A program may use at most 768 MiB of HBM per device.

v0:
```python
import functools
import math

import jax
import jax.numpy as jnp
from jax import lax
from jax.experimental import pallas as pl
from jax.experimental.pallas import tpu as pltpu
from jax.sharding import PartitionSpec as P

LANES = 128
SUBLANES = 8
HALF = SUBLANES // 2
TILES = 8
FEW = TILES // 2
ORDER = (4, 3, 2, 5, 1, 6, 7, 0)
MESH = pl.DeviceIdType.MESH


def bit_count(value, bits):
    total = value & 1
    for bit in range(1, bits):
        total = total + (jnp.right_shift(value, bit) & 1)
    return total


def butterfly(items, tan):
    items = list(items)
    span = 1
    while span < len(items):
        for low in range(len(items)):
            if not low & span:
                first, second = items[low], items[low + span]
                items[low] = first - tan * second
                items[low + span] = second + tan * first
        span *= 2
    return items


def turn(items):
    total = [None] * len(items)
    span = 1
    while span < len(items):
        for low in range(len(items)):
            if not low & span:
                first, second = items[low], items[low + span]
                total[low] = -second if total[low] is None else total[low] - second
                total[low + span] = first if total[low + span] is None else total[low + span] + first
        span *= 2
    return total


def row_index():
    return lax.broadcasted_iota(jnp.int32, (SUBLANES, LANES), 0)


def swap(value):
    return pltpu.roll(value, HALF, 0)


def row_partners(value, bit):
    step = 1 << bit
    down = pltpu.roll(value, step, 0)
    return down, down if 2 * step == SUBLANES else pltpu.roll(value, SUBLANES - step, 0)


def mix_rows(items, tan, bits):
    for bit in range(bits):
        high = jnp.right_shift(row_index(), bit) & 1 == 1
        factor = jnp.where(high, tan, -tan)
        mixed = []
        for item in items:
            down, up = row_partners(item, bit)
            mixed.append(item + factor * (down if down is up else jnp.where(high, down, up)))
        items = mixed
    return items


def turn_rows(items, totals, bits):
    for bit in range(bits):
        high = jnp.right_shift(row_index(), bit) & 1 == 1
        for place, item in enumerate(items):
            down, up = row_partners(item, bit)
            totals[place] = totals[place] + jnp.where(high, down, -up)
    return totals


def flip_lanes(items):
    square = jnp.concatenate(items, axis=0).T
    return [square[place * SUBLANES:(place + 1) * SUBLANES] for place in range(len(items))]


def kernel(layers, groups, qubits, cost_hbm, gamma_hbm, beta_hbm, terms_ref, real_ref, imag_ref,
           cost_ref, gamma_ref, beta_ref, cost_other, tan_buf, scale_buf, cos_buf, sin_buf, start_buf, turn_buf, work_buf,
           mixed_buf, send_buf, recv_buf, adj_buf, adj_send, adj_recv, sums, sums_mine, sums_all,
           send_sem, recv_sem, adj_send_sem, adj_recv_sem, cost_sem, sum_sem, in_sem):
    me = lax.axis_index('qx')
    chips = groups // 2
    chip, core = me // 2, me % 2
    other_core = chip * 2 + 1 - core
    vreg = (SUBLANES, LANES)
    slots = range(groups)
    last = layers - 1
    others = pl.ds(0, groups - 1)
    low_half = row_index() < HALF

    def rows(block):
        return pl.ds(block * SUBLANES, SUBLANES)

    def loop(count, body):
        lax.fori_loop(0, count, lambda step, carry: (body(step), carry)[1], 0)

    def at(step):
        off = ORDER[0]
        for place in range(1, chips):
            off = jnp.where(step == place, ORDER[place], off)
        there = lax.rem(chip + off, chips) * 2
        return [there, there + 1]

    def over_peers(body):
        @functools.partial(loop, chips - 1)
        def _(step):
            for peer in at(step):
                body(peer)

        body(other_core)

    def copy_to(peer, source, target, sends, recvs):
        pltpu.make_async_remote_copy(src_ref=source, dst_ref=target, send_sem=sends, recv_sem=recvs,
                                     device_id={'qx': peer}, device_id_type=MESH).start()

    def drain(view, sem):
        pltpu.make_async_copy(view, view, sem).wait()

    def angles(layer):
        half = jnp.full(vreg, beta_ref[layer], jnp.float32) * 0.5
        cos_half, sin_half = jnp.cos(half), jnp.sin(half)
        tan_buf[layer] = sin_half / cos_half
        scale = cos_half
        for digit in bin(qubits)[3:]:
            scale = scale * scale * (cos_half if digit == '1' else 1.0)
        scale_buf[layer] = scale

    def pack(dense, sign):
        moved = swap(dense)
        return jnp.where(low_half, dense, sign * moved), jnp.where(low_half, moved, sign * dense)

    def phases(layer, costs, scale):
        gamma = gamma_ref[layer]

        @functools.partial(loop, groups)
        def _(slot):
            for block in range(FEW):
                theta = gamma * costs[slot, rows(block)]
                for table, wave, sign in ((cos_buf, jnp.cos, 1.0), (sin_buf, jnp.sin, -1.0)):
                    table[layer, slot, 2 * block], table[layer, slot, 2 * block + 1] = pack(scale * wave(theta), sign)

    def ahead(layer, slot, tile, value):
        start_buf[layer, slot, tile] = value
        return value

    def phase(layer, slot, tile, value):
        return ahead(layer, slot, tile, cos_buf[layer, slot, tile] * value + sin_buf[layer, slot, tile] * swap(value))

    def unphase(layer, slot, tile, value):
        adj_buf[layer, slot, tile] = value
        return cos_buf[layer, slot, tile] * value - sin_buf[layer, slot, tile] * swap(value)

    def mix_slots(source, target, unit, tan):
        @functools.partial(loop, FEW)
        def _(step):
            tile = FEW * unit + step
            for slot, value in enumerate(butterfly([source[slot, tile] for slot in slots], tan)):
                target[slot, tile] = value

    def cross_even(unit, before, between, after):
        @functools.partial(loop, groups // 2)
        def _(step):
            for slot in (2 * step, 2 * step + 1):
                tiles = [FEW * unit + place for place in range(FEW)]
                values = [work_buf[slot, tile] for tile in tiles]
                if before is not None:
                    values = butterfly(values, before)
                values = between(slot, tiles, values)
                if after is not None:
                    for tile, value in zip(tiles, butterfly(values, after)):
                        work_buf[slot, tile] = value

        if after is not None:
            mix_slots(work_buf, mixed_buf, unit, after)

    def cross_odd(source, unit, before, between, after, send):
        tiles = (unit, unit + FEW)
        columns = [butterfly([source[slot, tile] for slot in slots], before) for tile in tiles]
        for slot in slots:
            pair = butterfly([column[slot] for column in columns], before)
            pair = butterfly([between(slot, tile, value) for tile, value in zip(tiles, pair)], after)
            columns[0][slot], columns[1][slot] = pair
        for tile, column in zip(tiles, columns):
            for slot, value in enumerate(butterfly(column, after)):
                send[slot, tile] = value

    def mix_common(peers, tiles, tan, source, send):
        items = [source[peer, tile] for peer in peers for tile in tiles]
        items = flip_lanes(mix_rows(items, tan, 2))
        items = flip_lanes(mix_rows(butterfly(items, tan), tan, 3))
        for place, peer in enumerate(peers):
            for offset, tile in enumerate(tiles):
                send[peer, tile] = items[len(tiles) * place + offset]

    def peers_of(steps, final):
        peers = []
        for step in steps:
            peers += at(2 * step) + at(2 * step + 1)
        peers[-2] = jnp.where(final, other_core, peers[-2])
        peers[-1] = jnp.where(final, me, peers[-1])
        return peers

    def depart_even(layer, unit, tan, send, recv, sends, recvs):
        tiles = [FEW * unit + place for place in range(FEW)]
        steps = chips // 2

        @functools.partial(loop, steps)
        def _(step):
            peers = peers_of([step], step == steps - 1)
            mix_common(peers, tiles, tan, mixed_buf, send)

            def go(peer):
                copy_to(peer, send.at[peer, pl.ds(0, FEW)], recv.at[me, pl.ds(0, FEW)], sends, recvs.at[0])

            @pl.when(unit == 0)
            def _():
                for peer in peers[:-1]:
                    go(peer)

            @pl.when(jnp.logical_and(unit == 0, step < steps - 1))
            def _():
                go(peers[-1])

        for tile in tiles:
            recv[me, tile] = send[me, tile]

        @pl.when(unit == 1)
        def _():
            @functools.partial(loop, FEW)
            def _(place):
                tile = FEW + place
                over_peers(lambda peer: copy_to(peer, send.at[peer, tile], recv.at[me, tile], sends, recvs.at[1 + place]))

    def depart_odd(unit, send, recv, sends, recvs):
        over_peers(lambda peer: copy_to(peer, send.at[peer, unit], recv.at[me, unit], sends, recvs.at[0]))
        for tile in (unit, unit + FEW):
            recv[me, tile] = send[me, tile]

        @pl.when(unit == FEW - 1)
        def _():
            over_peers(lambda peer: copy_to(peer, send.at[peer, pl.ds(FEW, FEW)], recv.at[me, pl.ds(FEW, FEW)], sends, recvs.at[1]))

    def mix_all(unit, tan, state):
        @functools.partial(loop, groups // 8)
        def _(step):
            for part in range(2):
                mix_common([8 * step + 4 * part + place for place in range(4)],
                           [FEW * unit + place for place in range(FEW)], tan, state, state)

    def arrive_even(unit, tan, recv, recvs):
        drain(recv.at[others, pl.ds(0, FEW)], recvs.at[unit])
        mix_all(unit, tan, recv)

    def arrive_odd(unit, recv, recvs):
        @pl.when(unit == 0)
        def _():
            drain(recv.at[others, pl.ds(0, FEW)], recvs.at[0])

        drain(recv.at[others, 0], recvs.at[1 + unit])

    def forward_of(layer):
        return tan_buf[layer], send_buf.at[layer], recv_buf.at[layer], send_sem.at[layer], recv_sem.at[layer]

    def backward_of(layer):
        return -tan_buf[layer], adj_send.at[layer], adj_recv.at[layer], adj_send_sem.at[layer], adj_recv_sem.at[layer]

    def turns(layer):
        @functools.partial(loop, TILES)
        def _(tile):
            for slot, value in enumerate(turn([start_buf[layer, slot, tile] for slot in slots])):
                turn_buf[layer, slot, tile] = value

        @functools.partial(loop, groups // 2)
        def _(step):
            places = [(2 * step + side, tile) for side in range(2) for tile in range(TILES)]
            items = [start_buf[layer, slot, tile] for slot, tile in places]
            totals = turn_rows(items, turn(items[:TILES]) + turn(items[TILES:]), 2)
            items = flip_lanes(items)
            items = flip_lanes(turn_rows(items, turn(items), 3))
            for place, (slot, tile) in enumerate(places):
                turn_buf[layer, slot, tile] = turn_buf[layer, slot, tile] + (totals[place] + items[place])

    over_peers(lambda peer: pl.semaphore_signal(
        pltpu.get_barrier_semaphore(), inc=1, device_id={'qx': peer}, device_id_type=MESH))
    loads = [pltpu.make_async_copy(source, target, in_sem.at[place]) for place, (source, target) in
             enumerate(((beta_hbm, beta_ref), (gamma_hbm, gamma_ref), (cost_hbm, cost_ref)))]
    for load in loads:
        load.start()
    sums_all[...] = jnp.zeros_like(sums_all)

    index_bits = bit_count(row_index() & (HALF - 1), 2) + bit_count(lax.broadcasted_iota(jnp.int32, vreg, 1), 7)
    quarter = (index_bits + bit_count(me, int(math.log2(groups)))) & 3

    def twist(slot, tile):
        now = (quarter + (bit_count(slot, int(math.log2(groups))) + bit_count(tile, 3))) & 3
        return (jnp.where(now == 0, 1.0, jnp.where(now == 2, -1.0, 0.0)),
                jnp.where(now == 1, 1.0, jnp.where(now == 3, -1.0, 0.0)))

    loads[0].wait()
    loop(layers, angles)
    loads[1].wait()
    loads[2].wait()
    phases(0, cost_ref, 2.0 ** (-qubits / 2))
    pl.semaphore_wait(pltpu.get_barrier_semaphore(), groups - 1)
    over_peers(lambda peer: copy_to(peer, cost_ref.at[peer], cost_other.at[me], cost_sem.at[0], cost_sem.at[1]))
    cost_other[me] = cost_ref[me]

    def begin(slot, tiles, values):
        values = []
        for tile in tiles:
            even, odd = twist(slot, tile)
            values.append(ahead(0, slot, tile, jnp.where(low_half, even, odd) * cos_buf[0, slot, tile]
                                + jnp.where(low_half, odd, even) * sin_buf[0, slot, tile]))
        return values

    @functools.partial(loop, 2)
    def _(unit):
        cross_even(unit, None, begin, tan_buf[0])
        depart_even(0, unit, *forward_of(0))

    drain(cost_other.at[others], cost_sem.at[1])
    phases(1, cost_other, scale_buf[0])
    turns(0)

    @functools.partial(loop, layers // 2)
    def _(pair):
        layer = 2 * pair + 1

        @functools.partial(loop, FEW)
        def _(unit):
            arrive_odd(unit, recv_buf.at[layer - 1], recv_sem.at[layer - 1])
            tan, *routes = forward_of(layer)
            cross_odd(recv_buf.at[layer - 1], unit, tan_buf[layer - 1], functools.partial(phase, layer), tan, routes[0])
            depart_odd(unit, *routes)

        @pl.when(layer < last)
        def _():
            phases(layer + 1, cost_ref, scale_buf[layer])

        turns(layer)

        @pl.when(layer < last)
        def _():
            even = layer + 1

            @functools.partial(loop, 2)
            def _(unit):
                arrive_even(unit, tan_buf[layer], recv_buf.at[layer], recv_sem.at[layer])
                mix_slots(recv_buf.at[layer], work_buf, unit, tan_buf[layer])
                cross_even(unit, tan_buf[layer], lambda slot, tiles, values: [
                    phase(even, slot, tile, value) for tile, value in zip(tiles, values)], tan_buf[even])
                depart_even(even, unit, *forward_of(even))

            phases(even + 1, cost_other, scale_buf[even])
            turns(even)

    sums[0] = jnp.zeros(vreg, jnp.float32)

    def middle(slot, tiles, values):
        scale = scale_buf[last]
        values = [scale * value for value in values]
        energy = sums[0]
        adjoint = []
        for pair in range(FEW // 2):
            block = tiles[2 * pair] // 2
            dense = pl.ds(pl.multiple_of(block * SUBLANES, SUBLANES), SUBLANES)
            final = []
            for tile, value in zip(tiles[2 * pair:2 * pair + 2], values[2 * pair:2 * pair + 2]):
                even, odd = twist(slot, tile)
                final.append(even * value + jnp.where(low_half, odd, -odd) * swap(value))
            real_ref[slot, dense] = jnp.where(low_half, final[0], swap(final[1]))
            imag_ref[slot, dense] = jnp.where(low_half, swap(final[0]), final[1])
            for cost, value in zip(pack(cost_ref[slot, dense], 1.0), values[2 * pair:2 * pair + 2]):
                turned = cost * value
                energy = energy + turned * value
                adjoint.append(scale * turned)
        sums[0] = energy
        return adjoint

    @functools.partial(loop, 2)
    def _(unit):
        arrive_even(unit, tan_buf[last], recv_buf.at[last], recv_sem.at[last])
        mix_slots(recv_buf.at[last], work_buf, unit, tan_buf[last])
        cross_even(unit, tan_buf[last], middle, -tan_buf[last])
        depart_even(last, unit, *backward_of(last))

    def slot_terms(layer, mixed):
        def one(tile, total):
            for slot, value in enumerate(turn([recv_buf[layer, slot, tile] for slot in slots])):
                total = total + mixed[slot, tile] * value
            return total

        sums[1 + layers + layer] = lax.fori_loop(0, TILES, one, jnp.zeros(vreg, jnp.float32))

    def start_terms(layer, costs):
        def one(slot, carry):
            gamma_sum, beta_sum = carry
            for block in range(FEW):
                for tile, cost in zip((2 * block, 2 * block + 1), pack(costs[slot, rows(block)], -1.0)):
                    adjoint = adj_buf[layer, slot, tile]
                    gamma_sum = gamma_sum + cost * (adjoint * swap(start_buf[layer, slot, tile]))
                    beta_sum = beta_sum + adjoint * turn_buf[layer, slot, tile]
            return gamma_sum, beta_sum

        zero = jnp.zeros(vreg, jnp.float32)
        gamma_sum, beta_sum = lax.fori_loop(0, groups, one, (zero, zero))
        sums[1 + layer] = 2.0 * gamma_sum
        sums[1 + layers + layer] = sums[1 + layers + layer] + beta_sum

    slot_terms(last, mixed_buf)

    @functools.partial(loop, groups)
    def _(slot):
        for block in range(FEW):
            for tile, cost in zip((2 * block, 2 * block + 1), pack(cost_ref[slot, rows(block)], -1.0)):
                adj_buf[0, slot, tile] = (2.0 * cost) * swap(start_buf[0, slot, tile])

    for state in (adj_buf.at[0], turn_buf.at[0]):
        @functools.partial(loop, 2)
        def _(unit):
            mix_all(unit, tan_buf[0], state)
            mix_slots(state, state, unit, tan_buf[0])

            @functools.partial(loop, groups)
            def _(slot):
                tiles = [FEW * unit + place for place in range(FEW)]
                for tile, value in zip(tiles, butterfly([state[slot, tile] for tile in tiles], tan_buf[0])):
                    state[slot, tile] = value


    @functools.partial(loop, layers // 2)
    def _(pair):
        layer = last - 2 * pair

        @functools.partial(loop, FEW)
        def _(unit):
            arrive_odd(unit, adj_recv.at[layer], adj_recv_sem.at[layer])
            tan, *routes = backward_of(layer - 1)
            cross_odd(adj_recv.at[layer], unit, -tan_buf[layer], functools.partial(unphase, layer), tan, routes[0])
            depart_odd(unit, *routes)

        slot_terms(layer - 1, adj_send.at[layer - 1])
        start_terms(layer, cost_other)

        @pl.when(layer > 1)
        def _():
            even = layer - 1

            @functools.partial(loop, 2)
            def _(unit):
                arrive_even(unit, -tan_buf[even], adj_recv.at[even], adj_recv_sem.at[even])
                mix_slots(adj_recv.at[even], work_buf, unit, -tan_buf[even])
                cross_even(unit, -tan_buf[even], lambda slot, tiles, values: [
                    unphase(even, slot, tile, value) for tile, value in zip(tiles, values)], -tan_buf[even - 1])
                depart_even(even - 1, unit, *backward_of(even - 1))

            slot_terms(even - 1, mixed_buf)
            start_terms(even, cost_ref)

    sums[1] = jnp.zeros(vreg, jnp.float32)

    def meet(unit):
        drain(adj_recv.at[0, others, pl.ds(0, FEW)], adj_recv_sem.at[0, unit])

        def one(slot, carry):
            gamma_sums, beta_sums = list(carry[:FEW]), list(carry[FEW:])
            for place in range(FEW):
                adjoint = adj_recv[0, slot, FEW * unit + place]
                gamma_sums[place] = gamma_sums[place] + adjoint * adj_buf[0, slot, FEW * unit + place]
                beta_sums[place] = beta_sums[place] + adjoint * turn_buf[0, slot, FEW * unit + place]
            return tuple(gamma_sums + beta_sums)

        values = lax.fori_loop(0, groups, one, tuple(jnp.zeros(vreg, jnp.float32) for _ in range(2 * FEW)))
        for term, parts in ((1, values[:FEW]), (1 + layers, values[FEW:])):
            sums[term] = sums[term] + ((parts[0] + parts[1]) + (parts[2] + parts[3]))

    lane = lax.broadcasted_iota(jnp.int32, vreg, 1)

    def gather(terms, mine):
        for term in terms:
            total = jnp.sum(jnp.sum(sums[term], axis=1, keepdims=True), axis=0, keepdims=True)
            place = jnp.logical_and(lane == max(term - 1, 0), row_index() == int(term == 0))
            mine = jnp.where(place, total, mine)
        return mine

    meet(0)
    late = (1, 1 + layers)
    sums_mine[...] = gather([term for term in range(1 + 2 * layers) if term not in late], jnp.zeros(vreg, jnp.float32))
    meet(1)
    mine = gather(late, sums_mine[...])
    sums_mine[...] = mine
    two = pl.ds(0, 2)
    over_peers(lambda peer: copy_to(peer, sums_mine.at[two], sums_all.at[me, two], sum_sem.at[0], sum_sem.at[1]))
    drain(sums_all.at[others, two], sum_sem.at[1])
    total = jnp.zeros(vreg, jnp.float32)
    for slot in slots:
        total = total + jnp.where(slot == me, mine, sums_all[slot])
    terms_ref[...] = total

    drain(cost_other.at[others], cost_sem.at[0])
    drain(sums_all.at[others, two], sum_sem.at[0])

    @functools.partial(loop, layers)
    def _(layer):
        drain(send_buf.at[layer, others], send_sem.at[layer])
        drain(adj_send.at[layer, others], adj_send_sem.at[layer])


def finish(terms_ref, real_in, imag_in, energy_ref, grad_ref, real_ref, imag_ref, energy_buf, grad_buf, sems):
    copies = [pltpu.make_async_copy(source, target, sems.at[place]) for place, (source, target) in enumerate((
        (real_in, real_ref), (imag_in, imag_ref), (energy_buf, energy_ref), (grad_buf, grad_ref)))]
    copies[0].start()
    copies[1].start()
    grad_buf[...] = terms_ref[0, :grad_buf.shape[0]]
    energy_buf[...] = terms_ref[1, :1]
    copies[2].start()
    copies[3].start()
    for copy in copies:
        copy.wait()


def solution(mesh):
    groups = mesh.shape['qx']

    def per_device(cost_flat, phase_angles, mixer_angles):
        chunk_len = cost_flat.shape[0]
        layers = phase_angles.shape[0]
        slot_rows = chunk_len // (groups * LANES)
        assert slot_rows == TILES * HALF and layers % 2 == 0 and groups == 2 * SUBLANES
        qubits = int(math.log2(chunk_len * groups))
        slots = (groups, slot_rows, LANES)
        vreg = (SUBLANES, LANES)
        state = (groups, TILES) + vreg
        states = (layers,) + state
        f32 = jnp.float32
        vmem = pl.BlockSpec(memory_space=pltpu.VMEM)
        hbm = pl.BlockSpec(memory_space=pltpu.HBM)
        dma = pltpu.SemaphoreType.DMA
        shape_of = jax.ShapeDtypeStruct
        results = pl.pallas_call(
            functools.partial(kernel, layers, groups, qubits),
            name='qaoa',
            out_shape=[shape_of(vreg, f32), shape_of(slots, f32), shape_of(slots, f32)],
            in_specs=[hbm] * 3,
            out_specs=[vmem] * 3,
            scratch_shapes=[
                pltpu.VMEM(slots, f32),
                pltpu.SMEM((layers,), f32),
                pltpu.SMEM((layers,), f32),
                pltpu.VMEM(slots, f32),
                pltpu.VMEM((layers,) + vreg, f32),
                pltpu.VMEM((layers,) + vreg, f32),
                pltpu.VMEM(states, f32),
                pltpu.VMEM(states, f32),
                pltpu.VMEM(states, f32),
                pltpu.VMEM(states, f32),
                pltpu.VMEM(state, f32),
                pltpu.VMEM(state, f32),
                pltpu.VMEM(states, f32),
                pltpu.VMEM(states, f32),
                pltpu.VMEM(states, f32),
                pltpu.VMEM(states, f32),
                pltpu.VMEM(states, f32),
                pltpu.VMEM((1 + 2 * layers,) + vreg, f32),
                pltpu.VMEM(vreg, f32),
                pltpu.VMEM((groups,) + vreg, f32),
                dma((layers,)), dma((layers, 1 + FEW)), dma((layers,)), dma((layers, 1 + FEW)),
                dma((2,)), dma((2,)), dma((3,)),
            ],
            compiler_params=pltpu.CompilerParams(
                collective_id=0, has_side_effects=True, vmem_limit_bytes=34 * 1024 * 1024),
        )(*(pltpu.with_memory_space_constraint(value, pltpu.HBM)
            for value in (cost_flat.reshape(slots), phase_angles, mixer_angles)))
        energy, grad, real, imag = pl.pallas_call(
            finish,
            name='finish',
            out_shape=[shape_of((1,), f32), shape_of((2 * layers,), f32), shape_of(slots, f32), shape_of(slots, f32)],
            in_specs=[vmem] * 3,
            out_specs=[hbm] * 4,
            scratch_shapes=[pltpu.VMEM((1,), f32), pltpu.VMEM((2 * layers,), f32), dma((4,))],
            compiler_params=pltpu.CompilerParams(vmem_limit_bytes=2 * 1024 * 1024),
        )(*results)
        return energy, grad, real.reshape(chunk_len), imag.reshape(chunk_len)

    return jax.shard_map(
        per_device, mesh=mesh, in_specs=(P(('inst', 'qx')), P(), P()),
        out_specs=(P('inst'), P('inst'), P(('inst', 'qx')), P(('inst', 'qx'))), check_vma=False)
```

profile of v0, /device:TPU:21, one launch (start us, length us, event | category | flops | bytes accessed | tf_op | source)
XLA Modules:
  0.0 166.3 jit_solution(16600831233282327871)
XLA Ops:
  0.6 164.8 %qaoa.1 = (f32[8,128]{1,0:T(8,128)S(1)}, f32[16,32,128]{2,1,0:T(8,128)S(1)}, f32[16,32,128]{2,1,0:T(8,128)S(1)}) custom-call(f32[16,32,128]{2,1,0:T(8,128)} %bitcast.3, f32[6]{0:T(128)} %gamma_hbm.1, f32[6]{0:T(128)} %beta_hbm.1), custom_call_target="tpu_custom_call" | custom-call | tf_op jit(solution)/shard_map/qaoa/pallas_call | solution.py:556
  165.4 0.8 finish.1
where the time goes:
time: 166 us
  Pallas kernels  166 us (100%)
    pallas_call x1, Pallas kernels, per_device(): pl.pallas_call(functools.partial(kernel, layers, groups, qubits), name='q...  165 us

commit v1 on v0

--- a/solution.py
+++ b/solution.py
@@ -189,7 +189,7 @@
         if after is not None:
             mix_slots(work_buf, mixed_buf, unit, after)
 
-    def cross_odd(source, unit, before, between, after, send):
+    def cross_odd(source, unit, before, between, after):
         tiles = (unit, unit + FEW)
         columns = [butterfly([source[slot, tile] for slot in slots], before) for tile in tiles]
         for slot in slots:
@@ -198,10 +198,10 @@
             columns[0][slot], columns[1][slot] = pair
         for tile, column in zip(tiles, columns):
             for slot, value in enumerate(butterfly(column, after)):
-                send[slot, tile] = value
-
-    def mix_common(peers, tiles, tan, source, send):
-        items = [source[peer, tile] for peer in peers for tile in tiles]
+                mixed_buf[slot, tile] = value
+
+    def mix_common(peers, tiles, tan, send):
+        items = [mixed_buf[peer, tile] for peer in peers for tile in tiles]
         items = flip_lanes(mix_rows(items, tan, 2))
         items = flip_lanes(mix_rows(butterfly(items, tan), tan, 3))
         for place, peer in enumerate(peers):
@@ -223,7 +223,7 @@
         @functools.partial(loop, steps)
         def _(step):
             peers = peers_of([step], step == steps - 1)
-            mix_common(peers, tiles, tan, mixed_buf, send)
+            mix_common(peers, tiles, tan, send)
 
             def go(peer):
                 copy_to(peer, send.at[peer, pl.ds(0, FEW)], recv.at[me, pl.ds(0, FEW)], sends, recvs.at[0])
@@ -247,25 +247,34 @@
                 tile = FEW + place
                 over_peers(lambda peer: copy_to(peer, send.at[peer, tile], recv.at[me, tile], sends, recvs.at[1 + place]))
 
-    def depart_odd(unit, send, recv, sends, recvs):
-        over_peers(lambda peer: copy_to(peer, send.at[peer, unit], recv.at[me, unit], sends, recvs.at[0]))
-        for tile in (unit, unit + FEW):
+    def depart_odd(layer, unit, tan, send, recv, sends, recvs):
+        tiles = (unit, unit + FEW)
+        steps = chips // 4
+
+        @functools.partial(loop, steps)
+        def _(step):
+            peers = peers_of([2 * step, 2 * step + 1], step == steps - 1)
+            mix_common(peers, tiles, tan, send)
+
+            def go(peer):
+                copy_to(peer, send.at[peer, unit], recv.at[me, unit], sends, recvs.at[0])
+
+            for peer in peers[:-1]:
+                go(peer)
+
+            @pl.when(step < steps - 1)
+            def _():
+                go(peers[-1])
+
+        for tile in tiles:
             recv[me, tile] = send[me, tile]
 
         @pl.when(unit == FEW - 1)
         def _():
             over_peers(lambda peer: copy_to(peer, send.at[peer, pl.ds(FEW, FEW)], recv.at[me, pl.ds(FEW, FEW)], sends, recvs.at[1]))
 
-    def mix_all(unit, tan, state):
-        @functools.partial(loop, groups // 8)
-        def _(step):
-            for part in range(2):
-                mix_common([8 * step + 4 * part + place for place in range(4)],
-                           [FEW * unit + place for place in range(FEW)], tan, state, state)
-
-    def arrive_even(unit, tan, recv, recvs):
+    def arrive_even(unit, recv, recvs):
         drain(recv.at[others, pl.ds(0, FEW)], recvs.at[unit])
-        mix_all(unit, tan, recv)
 
     def arrive_odd(unit, recv, recvs):
         @pl.when(unit == 0)
@@ -345,9 +354,8 @@
         @functools.partial(loop, FEW)
         def _(unit):
             arrive_odd(unit, recv_buf.at[layer - 1], recv_sem.at[layer - 1])
-            tan, *routes = forward_of(layer)
-            cross_odd(recv_buf.at[layer - 1], unit, tan_buf[layer - 1], functools.partial(phase, layer), tan, routes[0])
-            depart_odd(unit, *routes)
+            cross_odd(recv_buf.at[layer - 1], unit, tan_buf[layer - 1], functools.partial(phase, layer), tan_buf[layer])
+            depart_odd(layer, unit, *forward_of(layer))
 
         @pl.when(layer < last)
         def _():
@@ -361,7 +369,7 @@
 
             @functools.partial(loop, 2)
             def _(unit):
-                arrive_even(unit, tan_buf[layer], recv_buf.at[layer], recv_sem.at[layer])
+                arrive_even(unit, recv_buf.at[layer], recv_sem.at[layer])
                 mix_slots(recv_buf.at[layer], work_buf, unit, tan_buf[layer])
                 cross_even(unit, tan_buf[layer], lambda slot, tiles, values: [
                     phase(even, slot, tile, value) for tile, value in zip(tiles, values)], tan_buf[even])
@@ -395,15 +403,15 @@
 
     @functools.partial(loop, 2)
     def _(unit):
-        arrive_even(unit, tan_buf[last], recv_buf.at[last], recv_sem.at[last])
+        arrive_even(unit, recv_buf.at[last], recv_sem.at[last])
         mix_slots(recv_buf.at[last], work_buf, unit, tan_buf[last])
         cross_even(unit, tan_buf[last], middle, -tan_buf[last])
         depart_even(last, unit, *backward_of(last))
 
-    def slot_terms(layer, mixed):
+    def slot_terms(layer):
         def one(tile, total):
             for slot, value in enumerate(turn([recv_buf[layer, slot, tile] for slot in slots])):
-                total = total + mixed[slot, tile] * value
+                total = total + mixed_buf[slot, tile] * value
             return total
 
         sums[1 + layers + layer] = lax.fori_loop(0, TILES, one, jnp.zeros(vreg, jnp.float32))
@@ -423,7 +431,37 @@
         sums[1 + layer] = 2.0 * gamma_sum
         sums[1 + layers + layer] = sums[1 + layers + layer] + beta_sum
 
-    slot_terms(last, mixed_buf)
+    slot_terms(last)
+
+    @functools.partial(loop, layers // 2)
+    def _(pair):
+        layer = last - 2 * pair
+
+        @functools.partial(loop, FEW)
+        def _(unit):
+            arrive_odd(unit, adj_recv.at[layer], adj_recv_sem.at[layer])
+            cross_odd(adj_recv.at[layer], unit, -tan_buf[layer], functools.partial(unphase, layer), -tan_buf[layer - 1])
+            depart_odd(layer - 1, unit, *backward_of(layer - 1))
+
+        slot_terms(layer - 1)
+        start_terms(layer, cost_other)
+
+        @pl.when(layer > 1)
+        def _():
+            even = layer - 1
+
+            @functools.partial(loop, 2)
+            def _(unit):
+                arrive_even(unit, adj_recv.at[even], adj_recv_sem.at[even])
+                mix_slots(adj_recv.at[even], work_buf, unit, -tan_buf[even])
+                cross_even(unit, -tan_buf[even], lambda slot, tiles, values: [
+                    unphase(even, slot, tile, value) for tile, value in zip(tiles, values)], -tan_buf[even - 1])
+                depart_even(even - 1, unit, *backward_of(even - 1))
+
+            slot_terms(even - 1)
+            start_terms(even, cost_ref)
+
+    sums[1] = jnp.zeros(vreg, jnp.float32)
 
     @functools.partial(loop, groups)
     def _(slot):
@@ -431,62 +469,29 @@
             for tile, cost in zip((2 * block, 2 * block + 1), pack(cost_ref[slot, rows(block)], -1.0)):
                 adj_buf[0, slot, tile] = (2.0 * cost) * swap(start_buf[0, slot, tile])
 
-    for state in (adj_buf.at[0], turn_buf.at[0]):
-        @functools.partial(loop, 2)
-        def _(unit):
-            mix_all(unit, tan_buf[0], state)
-            mix_slots(state, state, unit, tan_buf[0])
-
-            @functools.partial(loop, groups)
-            def _(slot):
-                tiles = [FEW * unit + place for place in range(FEW)]
-                for tile, value in zip(tiles, butterfly([state[slot, tile] for tile in tiles], tan_buf[0])):
-                    state[slot, tile] = value
-
-
-    @functools.partial(loop, layers // 2)
-    def _(pair):
-        layer = last - 2 * pair
-
-        @functools.partial(loop, FEW)
-        def _(unit):
-            arrive_odd(unit, adj_recv.at[layer], adj_recv_sem.at[layer])
-            tan, *routes = backward_of(layer - 1)
-            cross_odd(adj_recv.at[layer], unit, -tan_buf[layer], functools.partial(unphase, layer), tan, routes[0])
-            depart_odd(unit, *routes)
-
-        slot_terms(layer - 1, adj_send.at[layer - 1])
-        start_terms(layer, cost_other)
-
-        @pl.when(layer > 1)
-        def _():
-            even = layer - 1
-
-            @functools.partial(loop, 2)
-            def _(unit):
-                arrive_even(unit, -tan_buf[even], adj_recv.at[even], adj_recv_sem.at[even])
-                mix_slots(adj_recv.at[even], work_buf, unit, -tan_buf[even])
-                cross_even(unit, -tan_buf[even], lambda slot, tiles, values: [
-                    unphase(even, slot, tile, value) for tile, value in zip(tiles, values)], -tan_buf[even - 1])
-                depart_even(even - 1, unit, *backward_of(even - 1))
-
-            slot_terms(even - 1, mixed_buf)
-            start_terms(even, cost_ref)
-
-    sums[1] = jnp.zeros(vreg, jnp.float32)
+    for source, target in ((adj_buf.at[0], work_buf), (turn_buf.at[0], mixed_buf)):
+        @functools.partial(loop, groups)
+        def _(slot):
+            for unit in range(2):
+                values = butterfly([source[slot, FEW * unit + place] for place in range(FEW)], tan_buf[0])
+                for place in range(FEW):
+                    source[slot, FEW * unit + place] = values[place]
+
+        for unit in range(2):
+            mix_slots(source, target, unit, tan_buf[0])
 
     def meet(unit):
-        drain(adj_recv.at[0, others, pl.ds(0, FEW)], adj_recv_sem.at[0, unit])
-
-        def one(slot, carry):
+        arrive_even(unit, adj_recv.at[0], adj_recv_sem.at[0])
+
+        def one(step, carry):
             gamma_sums, beta_sums = list(carry[:FEW]), list(carry[FEW:])
-            for place in range(FEW):
+            for slot, place in [(4 * step + side, place) for side in range(4) for place in range(FEW)]:
                 adjoint = adj_recv[0, slot, FEW * unit + place]
-                gamma_sums[place] = gamma_sums[place] + adjoint * adj_buf[0, slot, FEW * unit + place]
-                beta_sums[place] = beta_sums[place] + adjoint * turn_buf[0, slot, FEW * unit + place]
+                gamma_sums[place] = gamma_sums[place] + adjoint * work_buf[slot, FEW * unit + place]
+                beta_sums[place] = beta_sums[place] + adjoint * mixed_buf[slot, FEW * unit + place]
             return tuple(gamma_sums + beta_sums)
 
-        values = lax.fori_loop(0, groups, one, tuple(jnp.zeros(vreg, jnp.float32) for _ in range(2 * FEW)))
+        values = lax.fori_loop(0, groups // 4, one, tuple(jnp.zeros(vreg, jnp.float32) for _ in range(2 * FEW)))
         for term, parts in ((1, values[:FEW]), (1 + layers, values[FEW:])):
             sums[term] = sums[term] + ((parts[0] + parts[1]) + (parts[2] + parts[3]))
 
@@ -507,19 +512,20 @@
     sums_mine[...] = mine
     two = pl.ds(0, 2)
     over_peers(lambda peer: copy_to(peer, sums_mine.at[two], sums_all.at[me, two], sum_sem.at[0], sum_sem.at[1]))
-    drain(sums_all.at[others, two], sum_sem.at[1])
-    total = jnp.zeros(vreg, jnp.float32)
-    for slot in slots:
-        total = total + jnp.where(slot == me, mine, sums_all[slot])
-    terms_ref[...] = total
-
     drain(cost_other.at[others], cost_sem.at[0])
-    drain(sums_all.at[others, two], sum_sem.at[0])
 
     @functools.partial(loop, layers)
     def _(layer):
         drain(send_buf.at[layer, others], send_sem.at[layer])
         drain(adj_send.at[layer, others], adj_send_sem.at[layer])
+
+    drain(sums_all.at[others, two], sum_sem.at[1])
+    totals = [jnp.where(slot == me, mine, sums_all[slot]) for slot in slots]
+    while len(totals) > 1:
+        totals = [low + high for low, high in zip(totals[0::2], totals[1::2])]
+    terms_ref[...] = totals[0]
+
+    drain(sums_all.at[others, two], sum_sem.at[0])
 
 
 def finish(terms_ref, real_in, imag_in, energy_ref, grad_ref, real_ref, imag_ref, energy_buf, grad_buf, sems):

time: 166 us -> 164 us (0.988)
  Pallas kernels: 166 us -> 163 us
    pallas_call x1, Pallas kernels: 165 us -> 163 us  [per_device(): pl.pallas_call(functools.partial(kernel, layers, groups, qubits), name='q...]
where the time goes in v1:
time: 164 us
  Pallas kernels  163 us (99%)
    pallas_call x1, Pallas kernels, per_device(): pl.pallas_call(functools.partial(kernel, layers, groups, qubits), name='q...  163 us

profile of v1, /device:TPU:21, one launch (start us, length us, event | category | flops | bytes accessed | tf_op | source)
XLA Modules:
  0.0 164.0 jit_solution(7189268399192895793)
XLA Ops:
  0.6 162.5 %qaoa.1 = (f32[8,128]{1,0:T(8,128)S(1)}, f32[16,32,128]{2,1,0:T(8,128)S(1)}, f32[16,32,128]{2,1,0:T(8,128)S(1)}) custom-call(f32[16,32,128]{2,1,0:T(8,128)} %bitcast.3, f32[6]{0:T(128)} %gamma_hbm.1, f32[6]{0:T(128)} %beta_hbm.1), custom_call_target="tpu_custom_call" | custom-call | tf_op jit(solution)/shard_map/qaoa/pallas_call | solution.py:562
  163.2 0.8 finish.1

commit v2 on v1

--- a/solution.py
+++ b/solution.py
@@ -461,8 +461,6 @@
             slot_terms(even - 1)
             start_terms(even, cost_ref)
 
-    sums[1] = jnp.zeros(vreg, jnp.float32)
-
     @functools.partial(loop, groups)
     def _(slot):
         for block in range(FEW):
@@ -492,23 +490,23 @@
             return tuple(gamma_sums + beta_sums)
 
         values = lax.fori_loop(0, groups // 4, one, tuple(jnp.zeros(vreg, jnp.float32) for _ in range(2 * FEW)))
-        for term, parts in ((1, values[:FEW]), (1 + layers, values[FEW:])):
-            sums[term] = sums[term] + ((parts[0] + parts[1]) + (parts[2] + parts[3]))
+        return [(parts[0] + parts[1]) + (parts[2] + parts[3]) for parts in (values[:FEW], values[FEW:])]
 
     lane = lax.broadcasted_iota(jnp.int32, vreg, 1)
 
     def gather(terms, mine):
-        for term in terms:
-            total = jnp.sum(jnp.sum(sums[term], axis=1, keepdims=True), axis=0, keepdims=True)
+        for term, value in terms:
+            total = jnp.sum(jnp.sum(value, axis=0, keepdims=True), axis=1, keepdims=True)
             place = jnp.logical_and(lane == max(term - 1, 0), row_index() == int(term == 0))
             mine = jnp.where(place, total, mine)
         return mine
 
-    meet(0)
+    gamma_sum, beta_sum = meet(0)
     late = (1, 1 + layers)
-    sums_mine[...] = gather([term for term in range(1 + 2 * layers) if term not in late], jnp.zeros(vreg, jnp.float32))
-    meet(1)
-    mine = gather(late, sums_mine[...])
+    mine = gather([(term, sums[term]) for term in range(1 + 2 * layers) if term not in late], jnp.zeros(vreg, jnp.float32))
+    beta_sum = beta_sum + sums[1 + layers]
+    gamma_last, beta_last = meet(1)
+    mine = gather([(1, gamma_sum + gamma_last), (1 + layers, beta_sum + beta_last)], mine)
     sums_mine[...] = mine
     two = pl.ds(0, 2)
     over_peers(lambda peer: copy_to(peer, sums_mine.at[two], sums_all.at[me, two], sum_sem.at[0], sum_sem.at[1]))

time: 164 us -> 164 us (level)
  no operation moved by 1% of the time
where the time goes in v2:
time: 164 us
  Pallas kernels  163 us (99%)
    pallas_call x1, Pallas kernels, per_device(): pl.pallas_call(functools.partial(kernel, layers, groups, qubits), name='q...  163 us

profile of v2, /device:TPU:21, one launch (start us, length us, event | category | flops | bytes accessed | tf_op | source)
XLA Modules:
  0.0 164.0 jit_solution(11793396374847329779)
XLA Ops:
  0.6 162.5 %qaoa.1 = (f32[8,128]{1,0:T(8,128)S(1)}, f32[16,32,128]{2,1,0:T(8,128)S(1)}, f32[16,32,128]{2,1,0:T(8,128)S(1)}) custom-call(f32[16,32,128]{2,1,0:T(8,128)} %bitcast.3, f32[6]{0:T(128)} %gamma_hbm.1, f32[6]{0:T(128)} %beta_hbm.1), custom_call_target="tpu_custom_call" | custom-call | tf_op jit(solution)/shard_map/qaoa/pallas_call | solution.py:560
  163.2 0.8 finish.1
